TPU v7x, 32 devices: a whole 2x2x4 slice. The times are simulated.
32 devices in a mesh: ep: 8 (over y, x, core), tp: 4 (over z).
Axes of the slice: x: 2, y: 2, z: 4, core: 2. Of those that a mesh axis runs over, the one named last changes fastest.
Arguments:
- tokens: bfloat16 [1024, 2048], P('ep', 'tp'), may hold values from -6 to 6
- routing: int32 [1024, 8], P('ep'), may hold values from 0 to 31, all different within a row; in each aligned block of 128 rows (0 to 127, 128 to 255, ...) at most 64 rows name the same one
- gate_fixed: int32 [1024, 8], P('ep'), may hold values from 1 to 65535
- gate_weight: bfloat16 [32, 2048, 768], P('ep', 'tp'), may hold values from -0.125 to 0.125
- up_weight: bfloat16 [32, 2048, 768], P('ep', 'tp'), may hold values from -0.1875 to 0.1875
- down_weight: bfloat16 [32, 2048, 768], P('ep', 'tp'), may hold values from -0.21875 to 0.21875
Outputs:
- layer_out: bfloat16 [1024, 2048], P('ep', 'tp')
Inputs may be any that keep to these rules, and one draw needn't show every extreme that they name: `routing`: each token names 8 different experts. In each aligned block of 128 tokens (the tokens of one index of ep) no expert is named by more than 64 tokens, and in some blocks one expert is named by exactly 64.
All inputs are finite; a program needn't handle non-finite values.
Results may differ from a plain program's by a relative error of at most 0.0057.
Values may be sent and summed in bfloat16 or wider, within the bound.
A program may use at most 64 MiB of HBM per device.

v0:
```python
import functools

import jax
import jax.numpy as jnp
from jax import lax
from jax.experimental import pallas as pl
from jax.experimental.pallas import tpu as pltpu
from jax.sharding import PartitionSpec as P

MESH = pl.DeviceIdType.MESH
SKEW = 2


def layer_kernel(
    nep, n, local, cap, top,
    tok_ref, meta_ref, gw_hbm, uw_hbm, dw_hbm,
    out_ref,
    gw, uw, dw, tok_all, meta_all,
    ra, rb, ha, hb, pg, pu, acc, out_send, out_recv,
    w_sem, tok_s, tok_r, meta_s, meta_r,
    ra_s, ra_r, rb_s, rb_r, ha_s, ha_r, hb_s, hb_r, out_s, out_r,
):
    me = lax.axis_index("ep")
    z = lax.axis_index("tp")
    half = local // 2
    chunks = nep * half
    rows = tok_ref.shape[0]
    width = gw.shape[2]
    zl = lax.rem(z + n - 1, n)
    zr = lax.rem(z + 1, n)

    def weight_copy(i, e):
        src, dst = ((gw_hbm, gw), (uw_hbm, uw), (dw_hbm, dw))[i]
        return pltpu.make_async_copy(src.at[e], dst.at[e], w_sem.at[i, e])

    for i in ((0, 1), (2,)):
        for e in range(half):
            for first in (0, half):
                for which in i:
                    weight_copy(which, first + e).start()

    barrier = pltpu.get_barrier_semaphore()

    def greet(j, carry):
        pl.semaphore_signal(
            barrier, inc=1, device_id={"ep": lax.rem(me + j, nep)}, device_id_type=MESH
        )
        return carry

    lax.fori_loop(1, nep, greet, 0)

    for side in (zl, zr):
        pl.semaphore_signal(barrier, inc=1, device_id={"tp": side}, device_id_type=MESH)
    pl.semaphore_wait(barrier, nep + 1)

    def remote(src, dst, s, r, device):
        return pltpu.make_async_remote_copy(
            src_ref=src, dst_ref=dst, send_sem=s, recv_sem=r,
            device_id=device, device_id_type=MESH,
        )

    def tok_copy(j):
        to = {"ep": lax.rem(me - j + nep, nep)}
        return remote(tok_ref, tok_all.at[j], tok_s.at[j], tok_r.at[j], to)

    def meta_copy(j):
        to = {"ep": lax.rem(me - j + nep, nep)}
        return remote(meta_ref, meta_all.at[j], meta_s.at[j], meta_r.at[j], to)

    def out_copy(j):
        to = {"ep": lax.rem(me + j, nep)}
        return remote(out_send.at[j], out_recv.at[j], out_s.at[j], out_r.at[j], to)

    def ra_copy(k):
        return remote(ra.at[k], ra.at[k], ra_s.at[k], ra_r.at[k], {"tp": zl})

    def rb_copy(k):
        return remote(rb.at[k], rb.at[k], rb_s.at[k], rb_r.at[k], {"tp": zr})

    def ha_copy(k):
        return remote(ha.at[k], ha.at[k], ha_s.at[k], ha_r.at[k], {"tp": zr})

    def hb_copy(k):
        return remote(hb.at[k], hb.at[k], hb_s.at[k], hb_r.at[k], {"tp": zl})

    def send_tokens(j, carry):
        meta_copy(j).start()
        tok_copy(j).start()
        return carry

    lax.fori_loop(1, nep, send_tokens, 0)
    tok_all[0] = tok_ref[...]
    meta_all[0] = meta_ref[...]

    def clear(j, carry):
        acc[j] = jnp.zeros(acc.shape[1:], acc.dtype)
        return carry

    lax.fori_loop(0, nep, clear, 0)
    before = (
        lax.broadcasted_iota(jnp.int32, (rows, rows), 0)
        < lax.broadcasted_iota(jnp.int32, (rows, rows), 1)
    ).astype(jnp.bfloat16)
    slot_id = lax.broadcasted_iota(jnp.int32, (cap, rows), 0).astype(jnp.float32)

    def selection(j, e):
        named = meta_all[j, :top, :] == me * local + e
        chosen = jnp.sum(named.astype(jnp.float32), axis=0, keepdims=True)
        wide = jnp.broadcast_to(chosen, (16, rows)).astype(jnp.bfloat16)
        position = jnp.dot(wide, before, preferred_element_type=jnp.float32)[:1]
        hit = jnp.where(chosen > 0.5, position, -1.0)
        return named, slot_id == hit

    def gates(j, named, picked):
        values = meta_all[j, top:, :].astype(jnp.float32) / 65536.0
        row = jnp.sum(jnp.where(named, values, 0.0), axis=0, keepdims=True)
        return jnp.sum(jnp.where(picked, row, 0.0), axis=1, keepdims=True)

    def inside(k):
        return jnp.logical_and(k >= 0, k < chunks)

    def partial_stage(k, first_expert, buf, copy, has_source, is_last, hidden):
        @pl.when(inside(k))
        def _():
            j = k // half
            e = first_expert + k % half

            @pl.when(j == 0)
            def _():
                weight_copy(0, e).wait()
                weight_copy(1, e).wait()

            _, picked = selection(j, e)
            x = jnp.dot(
                picked.astype(jnp.bfloat16), tok_all[j], preferred_element_type=jnp.float32
            ).astype(jnp.bfloat16)
            pg[...] = jnp.dot(x, gw[e], preferred_element_type=jnp.float32)
            pu[...] = jnp.dot(x, uw[e], preferred_element_type=jnp.float32)

            @pl.when(has_source)
            def _():
                copy(k).wait_recv()
                pg[...] += buf[k, :, :width].astype(jnp.float32)
                pu[...] += buf[k, :, width:].astype(jnp.float32)

            @pl.when(jnp.logical_not(is_last))
            def _():
                buf[k, :, :width] = pg[...].astype(jnp.bfloat16)
                buf[k, :, width:] = pu[...].astype(jnp.bfloat16)
                copy(k).start()

            @pl.when(is_last)
            def _():
                v = pg[...]
                hidden[k] = (v / (1.0 + jnp.exp(-v)) * pu[...]).astype(jnp.bfloat16)

    def hidden_stage(k, first_expert, hidden, copy, has_source, is_last):
        @pl.when(inside(k))
        def _():
            @pl.when(has_source)
            def _():
                copy(k).wait_recv()

            @pl.when(jnp.logical_not(is_last))
            def _():
                copy(k).start()

            j = k // half
            e = first_expert + k % half

            @pl.when(j == 0)
            def _():
                weight_copy(2, e).wait()

            named, picked = selection(j, e)
            result = lax.dot_general(
                hidden[k], dw[e], (((1,), (1,)), ((), ())), preferred_element_type=jnp.float32
            )
            scaled = result * gates(j, named, picked)
            high = scaled.astype(jnp.bfloat16)
            low = (scaled - high.astype(jnp.float32)).astype(jnp.bfloat16)
            spread = picked.astype(jnp.bfloat16)
            acc[j] += lax.dot_general(
                jnp.concatenate([spread, spread], axis=0),
                jnp.concatenate([high, low], axis=0),
                (((0,), (0,)), ((), ())),
                preferred_element_type=jnp.float32,
            )

    turn = SKEW * (n - 1)
    from_right = SKEW * (n - 1 - z)
    from_left = SKEW * z

    def step(t, carry):
        k_first = t - jnp.minimum(from_left, from_right)

        @pl.when(jnp.logical_and(inside(k_first), k_first % half == 0))
        def _():
            j = k_first // half

            @pl.when(j > 0)
            def _():
                meta_copy(j).wait_recv()
                tok_copy(j).wait_recv()

        partial_stage(t - from_right, 0, ra, ra_copy, z < n - 1, z == 0, ha)
        partial_stage(t - from_left, half, rb, rb_copy, z > 0, z == n - 1, hb)
        hidden_stage(t - turn - from_left, 0, ha, ha_copy, z > 0, z == n - 1)
        hidden_stage(t - turn - from_right, half, hb, hb_copy, z < n - 1, z == 0)
        k_done = t - turn - jnp.maximum(from_left, from_right)

        @pl.when(jnp.logical_and(inside(k_done), k_done % half == half - 1))
        def _():
            j = k_done // half

            @pl.when(j > 0)
            def _():
                out_send[j] = acc[j].astype(jnp.bfloat16)
                out_copy(j).start()

        return carry

    lax.fori_loop(0, chunks + 2 * turn, step, 0)

    def finish_chunk(k, carry):
        @pl.when(z > 0)
        def _():
            ra_copy(k).wait_send()
            hb_copy(k).wait_send()

        @pl.when(z < n - 1)
        def _():
            rb_copy(k).wait_send()
            ha_copy(k).wait_send()

        return carry

    lax.fori_loop(0, chunks, finish_chunk, 0)

    def finish_block(j, carry):
        tok_copy(j).wait_send()
        meta_copy(j).wait_send()
        out_copy(j).wait_recv()
        acc[0] += out_recv[j].astype(jnp.float32)
        out_copy(j).wait_send()
        return carry

    lax.fori_loop(1, nep, finish_block, 0)
    out_ref[...] = acc[0].astype(jnp.bfloat16)


def on_device(nep, n, tokens, routing, gate_fixed, gate_weight, up_weight, down_weight):
    local, share, width = gate_weight.shape
    rows, top = routing.shape
    cap = max(2, rows * top * 2 // (local * nep))
    chunks = nep * (local // 2)
    meta = jnp.concatenate([routing.T, gate_fixed.T], axis=0)
    bf16, f32 = jnp.bfloat16, jnp.float32
    dma = pltpu.SemaphoreType.DMA
    vmem = pl.BlockSpec(memory_space=pltpu.VMEM)
    hbm = pl.BlockSpec(memory_space=pl.ANY)
    return pl.pallas_call(
        functools.partial(layer_kernel, nep, n, local, cap, top),
        out_shape=jax.ShapeDtypeStruct((rows, share), bf16),
        in_specs=[vmem, vmem, hbm, hbm, hbm],
        out_specs=vmem,
        scratch_shapes=[
            pltpu.VMEM((local, share, width), bf16),
            pltpu.VMEM((local, share, width), bf16),
            pltpu.VMEM((local, share, width), bf16),
            pltpu.VMEM((nep, rows, share), bf16),
            pltpu.VMEM((nep, 2 * top, rows), jnp.int32),
            pltpu.VMEM((chunks, cap, 2 * width), bf16),
            pltpu.VMEM((chunks, cap, 2 * width), bf16),
            pltpu.VMEM((chunks, cap, width), bf16),
            pltpu.VMEM((chunks, cap, width), bf16),
            pltpu.VMEM((cap, width), f32),
            pltpu.VMEM((cap, width), f32),
            pltpu.VMEM((nep, rows, share), f32),
            pltpu.VMEM((nep, rows, share), bf16),
            pltpu.VMEM((nep, rows, share), bf16),
            dma((3, local)),
            dma((nep,)), dma((nep,)), dma((nep,)), dma((nep,)),
            dma((chunks,)), dma((chunks,)), dma((chunks,)), dma((chunks,)),
            dma((chunks,)), dma((chunks,)), dma((chunks,)), dma((chunks,)),
            dma((nep,)), dma((nep,)),
        ],
        compiler_params=pltpu.CompilerParams(
            collective_id=0, has_side_effects=True, vmem_limit_bytes=60 * 1024 * 1024
        ),
    )(tokens, meta, gate_weight, up_weight, down_weight)


def solution(mesh):
    in_specs = (
        P("ep", "tp"),
        P("ep", None),
        P("ep", None),
        P("ep", "tp", None),
        P("ep", "tp", None),
        P("ep", "tp", None),
    )
    body = functools.partial(on_device, mesh.shape["ep"], mesh.shape["tp"])
    return jax.shard_map(
        body, mesh=mesh, in_specs=in_specs, out_specs=P("ep", "tp"), check_vma=False
    )
```

profile of v0, /device:TPU:1, one launch (start us, length us, event | category | flops | bytes accessed | tf_op | source)
XLA Modules:
  0.0 138.4 jit_solution(16980456115657084440)
XLA Ops:
  0.0 1.3 pad_add_fusion.meta_ref
  1.3 135.5 %shard_map.64 = bf16[128,512]{1,0:T(8,128)(2,1)} custom-call(bf16[128,512]{1,0:T(8,128)(2,1)} %tok_ref.1, s32[16,128]{1,0:T(8,128)} %pad_add_fusion.meta_ref, bf16[4,512,768]{2,1,0:T(8,128)(2,1)} %gw_hbm.1, bf16[4,512,768]{2,1,0:T(8,128)(2,1)} %uw_hbm.1, bf16[4,512,768]{2,1,0:T(8,128)(2,1)} %dw_hbm.1), custom_call_target="tpu_custom_call" | custom-call | tf_op jit(solution)/shard_map/pallas_call | solution.py:262
  136.8 1.6 %copy.8 = bf16[128,512]{1,0:T(8,128)(2,1)} copy(bf16[128,512]{1,0:T(8,128)(2,1)} %shard_map.64) | data formatting | bytes 262144
where the time goes:
time: 139 us; the launch traced here: 138 us
  Pallas kernels  136 us (98%)
  local copies, waits for them, and re-layouts  1.57 us (1%)
    pallas_call x1, Pallas kernels, on_device(): pl.pallas_call(functools.partial(layer_kernel, nep, n, local, cap, top),...  136 us

commit v1 on v0

v1 whole, which is shorter than its diff:
```python
import functools

import jax
import jax.numpy as jnp
from jax import lax
from jax.experimental import pallas as pl
from jax.experimental.pallas import tpu as pltpu
from jax.sharding import PartitionSpec as P

MESH = pl.DeviceIdType.MESH
SKEW = 2
GROUPS = 4
LANES = 128


def layer_kernel(
    nep, n, local, top, nq, half,
    tok_ref, meta_ref, gw_hbm, uw_hbm, dw_hbm,
    out_ref,
    gu, dw, tok_all, meta_all, place, ghi, glo, ends,
    xbuf, own, ra, rb, ha, hb, acc, out_send, out_recv,
    gu_sem, dw_sem, tok_s, tok_r, meta_s, meta_r,
    ra_s, ra_r, rb_s, rb_r, ha_s, ha_r, hb_s, hb_r, out_s, out_r,
):
    me = lax.axis_index("ep")
    z = lax.axis_index("tp")
    rows = tok_ref.shape[0]
    nb = nep // nq
    span = nb * rows
    ng = gu.shape[0]
    chunks = nq * ng
    bf16, f32 = jnp.bfloat16, jnp.float32
    zl = lax.rem(z + n - 1, n)
    zr = lax.rem(z + 1, n)
    my_group = me // nb
    my_slot = lax.rem(me, nb)

    def gate_copy(g):
        return pltpu.make_async_copy(
            gw_hbm.at[:, :, pl.ds(g * LANES, LANES)],
            gu.at[g, :, :, pl.ds(0, LANES)], gu_sem.at[0, g],
        )

    def up_copy(g):
        return pltpu.make_async_copy(
            uw_hbm.at[:, :, pl.ds(g * LANES, LANES)],
            gu.at[g, :, :, pl.ds(LANES, LANES)], gu_sem.at[1, g],
        )

    down_copy = pltpu.make_async_copy(dw_hbm, dw, dw_sem)

    for g in range(ng):
        gate_copy(g).start()
        up_copy(g).start()
    down_copy.start()

    barrier = pltpu.get_barrier_semaphore()

    def greet(j, carry):
        pl.semaphore_signal(
            barrier, inc=1, device_id={"ep": lax.rem(me + j, nep)}, device_id_type=MESH
        )
        return carry

    lax.fori_loop(1, nep, greet, 0)
    for side in (zl, zr):
        pl.semaphore_signal(barrier, inc=1, device_id={"tp": side}, device_id_type=MESH)
    pl.semaphore_wait(barrier, nep + 1)

    def remote(src, dst, s, r, device):
        return pltpu.make_async_remote_copy(
            src_ref=src, dst_ref=dst, send_sem=s, recv_sem=r,
            device_id=device, device_id_type=MESH,
        )

    def block_of(i):
        return pl.ds(pl.multiple_of(i * rows, rows), rows)

    def tok_copy(m):
        to = lax.rem(my_group - m // nb + nq, nq) * nb + lax.rem(m, nb)
        slot = (m // nb) * nb + my_slot
        return remote(
            tok_ref, tok_all.at[m // nb, block_of(my_slot), :], tok_s.at[m], tok_r.at[slot],
            {"ep": to},
        )

    def meta_copy(m):
        to = lax.rem(my_group - m // nb + nq, nq) * nb + lax.rem(m, nb)
        slot = (m // nb) * nb + my_slot
        return remote(
            meta_ref, meta_all.at[m // nb, :, block_of(my_slot)], meta_s.at[m], meta_r.at[slot],
            {"ep": to},
        )

    def tok_arrival(m):
        return remote(
            tok_ref, tok_all.at[m // nb, block_of(lax.rem(m, nb)), :], tok_s.at[m], tok_r.at[m],
            {"ep": lax.rem(me + 1, nep)},
        )

    def meta_arrival(m):
        return remote(
            meta_ref, meta_all.at[m // nb, :, block_of(lax.rem(m, nb))], meta_s.at[m],
            meta_r.at[m], {"ep": lax.rem(me + 1, nep)},
        )

    def out_copy(m):
        to = lax.rem(my_group + m // nb, nq) * nb + lax.rem(m, nb)
        return remote(
            out_send.at[m // nb, block_of(lax.rem(m, nb)), :], out_recv.at[me],
            out_s.at[m], out_r.at[me], {"ep": to},
        )

    def out_arrival(j):
        source = lax.rem(me + j, nep)
        return source, remote(
            out_send.at[0, block_of(0), :], out_recv.at[source],
            out_s.at[0], out_r.at[source], {"ep": source},
        )

    def ra_copy(k):
        return remote(ra.at[k], ra.at[k], ra_s.at[k], ra_r.at[k], {"tp": zl})

    def rb_copy(k):
        return remote(rb.at[k], rb.at[k], rb_s.at[k], rb_r.at[k], {"tp": zr})

    def ha_copy(k):
        return remote(ha.at[k], ha.at[k], ha_s.at[k], ha_r.at[k], {"tp": zr})

    def hb_copy(k):
        return remote(hb.at[k], hb.at[k], hb_s.at[k], hb_r.at[k], {"tp": zl})

    def send_tokens(m, carry):
        @pl.when(m != my_slot)
        def _():
            meta_copy(m).start()
            tok_copy(m).start()

        return carry

    lax.fori_loop(0, nep, send_tokens, 0)
    tok_all[0, block_of(my_slot), :] = tok_ref[...]
    meta_all[0, :, block_of(my_slot)] = meta_ref[...]

    def clear(j, carry):
        acc[j] = jnp.zeros(acc.shape[1:], acc.dtype)
        return carry

    lax.fori_loop(0, nq, clear, 0)

    before = (
        lax.broadcasted_iota(jnp.int32, (span, span), 0)
        < lax.broadcasted_iota(jnp.int32, (span, span), 1)
    ).astype(bf16)
    row_id = lax.broadcasted_iota(jnp.int32, (half, span), 0).astype(f32)
    row_col = lax.broadcasted_iota(jnp.int32, (half, LANES), 0).astype(f32)
    sub_id = lax.broadcasted_iota(jnp.int32, (16, span), 0)

    def prepare(q):
        def arrive(i, carry):
            m = q * nb + i

            @pl.when(m != my_slot)
            def _():
                meta_arrival(m).wait_recv()
                tok_arrival(m).wait_recv()

            return carry

        lax.fori_loop(0, nb, arrive, 0)
        ids = meta_all[q, :top, :]
        fixed = meta_all[q, top:, :]
        chosen, wide = [], jnp.zeros((16, span), f32)
        for e in range(local):
            named = ids == me * local + e
            row = jnp.sum(named.astype(f32), axis=0, keepdims=True)
            gate = jnp.sum(jnp.where(named, fixed, 0), axis=0, keepdims=True)
            high = gate // 256
            ghi[q, e:e + 1, :] = (high * 256).astype(f32)
            glo[q, e:e + 1, :] = (gate - high * 256).astype(f32)
            wide = jnp.where(sub_id == e, row, wide)
            chosen.append(row)
        earlier = jnp.dot(wide.astype(bf16), before, preferred_element_type=f32)
        base = jnp.zeros((1, 1), f32)
        for e in range(local):
            place[q, e:e + 1, :] = jnp.where(
                chosen[e] > 0.5, base + earlier[e:e + 1, :], -1.0
            )
            base = base + jnp.sum(chosen[e], axis=1, keepdims=True)
            ends[q, e:e + 1, :] = jnp.broadcast_to(base, (1, LANES))

    def inside(k):
        return jnp.logical_and(k >= 0, k < chunks)

    def partial_stage(k, d, buf, copy, has_source, is_last, hidden):
        @pl.when(inside(k))
        def _():
            q = k // ng
            g = lax.rem(k, ng)

            @pl.when(g == 0)
            def _():
                for e in range(local):
                    pick = (row_id + float(d * half)) == place[q, e:e + 1, :]
                    xbuf[d, e] = jnp.dot(
                        pick.astype(bf16), tok_all[q], preferred_element_type=f32
                    ).astype(bf16)

            total = jnp.dot(xbuf[d, 0], gu[g, 0], preferred_element_type=f32)
            for e in range(1, local):
                total += jnp.dot(xbuf[d, e], gu[g, e], preferred_element_type=f32)
            own[...] = total

            @pl.when(has_source)
            def _():
                copy(k).wait_recv()
                own[...] += buf[k].astype(f32)

            @pl.when(jnp.logical_not(is_last))
            def _():
                buf[k] = own[...].astype(bf16)
                copy(k).start()

            @pl.when(is_last)
            def _():
                v = own[:, :LANES]
                hidden[k] = (v / (1.0 + jnp.exp(-v)) * own[:, LANES:]).astype(bf16)

    def hidden_stage(k, d, hidden, copy, has_source, is_last):
        @pl.when(inside(k))
        def _():
            @pl.when(has_source)
            def _():
                copy(k).wait_recv()

            @pl.when(jnp.logical_not(is_last))
            def _():
                copy(k).start()

            q = k // ng

            @pl.when(lax.rem(k, ng) == ng - 1)
            def _():
                units = jnp.concatenate([hidden[q * ng + g] for g in range(ng)], axis=1)
                at = row_col + float(d * half)
                start = jnp.zeros((1, LANES), f32)
                result = jnp.zeros((half, dw.shape[1]), f32)
                high = jnp.zeros((half, span), f32)
                low = jnp.zeros((half, span), f32)
                for e in range(local):
                    end = ends[q, e:e + 1, :]
                    mine = jnp.logical_and(at >= start, at < end).astype(f32).astype(bf16)
                    start = end
                    result += lax.dot_general(
                        units * jnp.concatenate([mine] * ng, axis=1), dw[e],
                        (((1,), (1,)), ((), ())), preferred_element_type=f32,
                    )
                    pick = (row_id + float(d * half)) == place[q, e:e + 1, :]
                    high = jnp.where(pick, ghi[q, e:e + 1, :], high)
                    low = jnp.where(pick, glo[q, e:e + 1, :], low)
                rounded = result.astype(bf16)
                acc[q] += lax.dot_general(
                    jnp.concatenate([high.astype(bf16), low.astype(bf16)], axis=0),
                    jnp.concatenate([rounded, rounded], axis=0),
                    (((0,), (0,)), ((), ())), preferred_element_type=f32,
                )

    turn = SKEW * (n - 1)
    from_right = SKEW * (n - 1 - z)
    from_left = SKEW * z
    lead = jnp.minimum(from_left, from_right)

    def step(t, carry):
        k_first = t - lead

        @pl.when(jnp.logical_and(inside(k_first), lax.rem(k_first, ng) == 0))
        def _():
            prepare(k_first // ng)

        @pl.when(jnp.logical_and(k_first >= 0, k_first < ng))
        def _():
            gate_copy(k_first).wait()
            up_copy(k_first).wait()

        @pl.when(t == turn + lead)
        def _():
            down_copy.wait()

        partial_stage(t - from_right, 0, ra, ra_copy, z < n - 1, z == 0, ha)
        partial_stage(t - from_left, 1, rb, rb_copy, z > 0, z == n - 1, hb)
        hidden_stage(t - turn - from_left, 0, ha, ha_copy, z > 0, z == n - 1)
        hidden_stage(t - turn - from_right, 1, hb, hb_copy, z < n - 1, z == 0)
        k_done = t - turn - jnp.maximum(from_left, from_right)

        @pl.when(jnp.logical_and(inside(k_done), lax.rem(k_done, ng) == ng - 1))
        def _():
            q = k_done // ng
            out_send[q] = (acc[q] * (1.0 / 65536.0)).astype(bf16)

            def give(i, carry):
                m = q * nb + i

                @pl.when(m != my_slot)
                def _():
                    out_copy(m).start()

                return carry

            lax.fori_loop(0, nb, give, 0)

        return carry

    lax.fori_loop(0, chunks + 2 * turn, step, 0)

    def finish_chunk(k, carry):
        @pl.when(z > 0)
        def _():
            ra_copy(k).wait_send()
            hb_copy(k).wait_send()

        @pl.when(z < n - 1)
        def _():
            rb_copy(k).wait_send()
            ha_copy(k).wait_send()

        return carry

    lax.fori_loop(0, chunks, finish_chunk, 0)

    def finish_send(m, carry):
        @pl.when(m != my_slot)
        def _():
            tok_copy(m).wait_send()
            meta_copy(m).wait_send()
            out_copy(m).wait_send()

        return carry

    lax.fori_loop(0, nep, finish_send, 0)
    own_rows = block_of(my_slot)
    acc[0, own_rows, :] = acc[0, own_rows, :] * (1.0 / 65536.0)

    def finish_block(j, carry):
        source, copy = out_arrival(j)
        copy.wait_recv()
        acc[0, own_rows, :] += out_recv[source].astype(f32)
        return carry

    lax.fori_loop(1, nep, finish_block, 0)
    out_ref[...] = acc[0, own_rows, :].astype(bf16)


def on_device(nep, n, tokens, routing, gate_fixed, gate_weight, up_weight, down_weight):
    local, share, width = gate_weight.shape
    rows, top = routing.shape
    cap = max(2, rows * top * 2 // (local * nep))
    nq = min(GROUPS, nep)
    nb = nep // nq
    half = nb * local * cap // 2
    ng = width // LANES
    chunks = nq * ng
    meta = jnp.concatenate([routing.T, gate_fixed.T], axis=0)
    bf16, f32 = jnp.bfloat16, jnp.float32
    dma = pltpu.SemaphoreType.DMA
    vmem = pl.BlockSpec(memory_space=pltpu.VMEM)
    hbm = pl.BlockSpec(memory_space=pl.ANY)
    return pl.pallas_call(
        functools.partial(layer_kernel, nep, n, local, top, nq, half),
        out_shape=jax.ShapeDtypeStruct((rows, share), bf16),
        in_specs=[vmem, vmem, hbm, hbm, hbm],
        out_specs=vmem,
        scratch_shapes=[
            pltpu.VMEM((ng, local, share, 2 * LANES), bf16),
            pltpu.VMEM((local, share, width), bf16),
            pltpu.VMEM((nq, nb * rows, share), bf16),
            pltpu.VMEM((nq, 2 * top, nb * rows), jnp.int32),
            pltpu.VMEM((nq, 8, nb * rows), f32),
            pltpu.VMEM((nq, 8, nb * rows), f32),
            pltpu.VMEM((nq, 8, nb * rows), f32),
            pltpu.VMEM((nq, 8, LANES), f32),
            pltpu.VMEM((2, local, half, share), bf16),
            pltpu.VMEM((half, 2 * LANES), f32),
            pltpu.VMEM((chunks, half, 2 * LANES), bf16),
            pltpu.VMEM((chunks, half, 2 * LANES), bf16),
            pltpu.VMEM((chunks, half, LANES), bf16),
            pltpu.VMEM((chunks, half, LANES), bf16),
            pltpu.VMEM((nq, nb * rows, share), f32),
            pltpu.VMEM((nq, nb * rows, share), bf16),
            pltpu.VMEM((nep, rows, share), bf16),
            dma((2, ng)), dma,
            dma((nep,)), dma((nep,)), dma((nep,)), dma((nep,)),
            dma((chunks,)), dma((chunks,)), dma((chunks,)), dma((chunks,)),
            dma((chunks,)), dma((chunks,)), dma((chunks,)), dma((chunks,)),
            dma((nep,)), dma((nep,)),
        ],
        compiler_params=pltpu.CompilerParams(
            collective_id=0, has_side_effects=True, vmem_limit_bytes=60 * 1024 * 1024
        ),
    )(tokens, meta, gate_weight, up_weight, down_weight)


def solution(mesh):
    in_specs = (
        P("ep", "tp"),
        P("ep", None),
        P("ep", None),
        P("ep", "tp", None),
        P("ep", "tp", None),
        P("ep", "tp", None),
    )
    body = functools.partial(on_device, mesh.shape["ep"], mesh.shape["tp"])
    return jax.shard_map(
        body, mesh=mesh, in_specs=in_specs, out_specs=P("ep", "tp"), check_vma=False
    )
```

time: 139 us -> 141 us (1.014)
  Pallas kernels: 136 us -> 138 us
    pallas_call x1, Pallas kernels: 136 us -> 138 us  [on_device(): pl.pallas_call(functools.partial(layer_kernel, nep, n, local, top, nq, ha...]
where the time goes in v1:
time: 141 us
  Pallas kernels  138 us (98%)
  local copies, waits for them, and re-layouts  1.57 us (1%)
    pallas_call x1, Pallas kernels, on_device(): pl.pallas_call(functools.partial(layer_kernel, nep, n, local, top, nq, ha...  138 us

profile of v1, /device:TPU:1, one launch (start us, length us, event | category | flops | bytes accessed | tf_op | source)
XLA Modules:
  0.0 140.9 jit_solution(17602122717366533305)
XLA Ops:
  0.0 1.3 pad_add_fusion.meta_ref
  1.3 138.0 %shard_map.64 = bf16[128,512]{1,0:T(8,128)(2,1)} custom-call(bf16[128,512]{1,0:T(8,128)(2,1)} %tok_ref.1, s32[16,128]{1,0:T(8,128)} %pad_add_fusion.meta_ref, bf16[4,512,768]{2,1,0:T(8,128)(2,1)} %gw_hbm.1, bf16[4,512,768]{2,1,0:T(8,128)(2,1)} %uw_hbm.1, bf16[4,512,768]{2,1,0:T(8,128)(2,1)} %dw_hbm.1), custom_call_target="tpu_custom_call" | custom-call | tf_op jit(solution)/shard_map/pallas_call | solution.py:367
  139.3 1.6 %copy.8 = bf16[128,512]{1,0:T(8,128)(2,1)} copy(bf16[128,512]{1,0:T(8,128)(2,1)} %shard_map.64) | data formatting | bytes 262144

commit v2 on v1

v2 whole, which is shorter than its diff:
```python
import functools

import jax
import jax.numpy as jnp
from jax import lax
from jax.experimental import pallas as pl
from jax.experimental.pallas import tpu as pltpu
from jax.sharding import PartitionSpec as P

MESH = pl.DeviceIdType.MESH
SKEW = 2
GROUPS = 4
LANES = 128
SIZES = (10, 11)


def remote(src, dst, s, r, device):
    return pltpu.make_async_remote_copy(
        src_ref=src, dst_ref=dst, send_sem=s, recv_sem=r,
        device_id=device, device_id_type=MESH,
    )


def count_kernel(
    nep, nq, local, top, limits,
    meta_ref, all_ref, size_ref, meta_all, meta_s, meta_r,
):
    me = lax.axis_index("ep")
    rows = meta_ref.shape[1]
    nb = nep // nq
    my_group = me // nb
    my_slot = lax.rem(me, nb)
    barrier = pltpu.get_barrier_semaphore()

    def greet(j, carry):
        pl.semaphore_signal(
            barrier, inc=1, device_id={"ep": lax.rem(me + j, nep)}, device_id_type=MESH
        )
        return carry

    lax.fori_loop(1, nep, greet, 0)
    pl.semaphore_wait(barrier, nep - 1)

    def block_of(i):
        return pl.ds(pl.multiple_of(i * rows, rows), rows)

    def give(m):
        to = lax.rem(my_group - m // nb + nq, nq) * nb + lax.rem(m, nb)
        slot = (m // nb) * nb + my_slot
        return remote(
            meta_ref, meta_all.at[m // nb, :, block_of(my_slot)], meta_s.at[m], meta_r.at[slot],
            {"ep": to},
        )

    def arrival(m):
        return remote(
            meta_ref, meta_all.at[m // nb, :, block_of(lax.rem(m, nb))], meta_s.at[m],
            meta_r.at[m], {"ep": lax.rem(me + 1, nep)},
        )

    def start(m, carry):
        @pl.when(m != my_slot)
        def _():
            give(m).start()

        return carry

    def finish(m, carry):
        @pl.when(m != my_slot)
        def _():
            arrival(m).wait_recv()

        return carry

    def sent(m, carry):
        @pl.when(m != my_slot)
        def _():
            give(m).wait_send()

        return carry

    lax.fori_loop(0, nep, start, 0)
    meta_all[0, :, block_of(my_slot)] = meta_ref[...]
    lax.fori_loop(0, nep, finish, 0)
    worst = jnp.zeros((1, 1), jnp.float32)
    for q in range(nq):
        ids = meta_all[q, :top, :]
        all_ref[q] = meta_all[q]
        for c in range(nep // 2):
            here = jnp.logical_and(ids >= c * 2 * local, ids < (c + 1) * 2 * local)
            row = jnp.sum(here.astype(jnp.float32), axis=0, keepdims=True)
            worst = jnp.maximum(worst, jnp.sum(row, axis=1, keepdims=True))
    top_load = jnp.max(worst)
    size = jnp.int32(0)
    for limit in limits:
        size += (top_load > float(limit)).astype(jnp.int32)
    size_ref[0] = size
    lax.fori_loop(0, nep, sent, 0)


def layer_kernel(
    nep, n, local, top, nq, full, half,
    tok_ref, meta_all, gw_hbm, uw_hbm, dw_hbm,
    out_ref,
    gu, dw, tok_all, place, gate, ends,
    xbuf, own, ra, rb, ha, hb, sp_out, sp_in, hs_in, acc, out_send, out_recv,
    gu_sem, dw_sem, tok_s, tok_r,
    ra_s, ra_r, rb_s, rb_r, ha_s, ha_r, hb_s, hb_r, sp_s, sp_r, hs_s, hs_r, out_s, out_r,
):
    me = lax.axis_index("ep")
    z = lax.axis_index("tp")
    spill = full - half
    low_row = half - spill
    partner = me + 1 - 2 * lax.rem(me, 2)
    rows = tok_ref.shape[0]
    nb = nep // nq
    span = nb * rows
    ng = gu.shape[0]
    chunks = nq * ng
    bf16, f32 = jnp.bfloat16, jnp.float32
    zl = lax.rem(z + n - 1, n)
    zr = lax.rem(z + 1, n)
    my_group = me // nb
    my_slot = lax.rem(me, nb)

    def gate_copy(g):
        return pltpu.make_async_copy(
            gw_hbm.at[:, :, pl.ds(g * LANES, LANES)],
            gu.at[g, :, :, pl.ds(0, LANES)], gu_sem.at[0, g],
        )

    def up_copy(g):
        return pltpu.make_async_copy(
            uw_hbm.at[:, :, pl.ds(g * LANES, LANES)],
            gu.at[g, :, :, pl.ds(LANES, LANES)], gu_sem.at[1, g],
        )

    down_copy = pltpu.make_async_copy(dw_hbm, dw, dw_sem)

    for g in range(ng):
        gate_copy(g).start()
        up_copy(g).start()
    down_copy.start()

    barrier = pltpu.get_barrier_semaphore()

    def greet(j, carry):
        pl.semaphore_signal(
            barrier, inc=1, device_id={"ep": lax.rem(me + j, nep)}, device_id_type=MESH
        )
        return carry

    lax.fori_loop(1, nep, greet, 0)
    for side in (zl, zr):
        pl.semaphore_signal(barrier, inc=1, device_id={"tp": side}, device_id_type=MESH)
    pl.semaphore_wait(barrier, nep + 1)

    def block_of(i):
        return pl.ds(pl.multiple_of(i * rows, rows), rows)

    def tok_copy(m):
        to = lax.rem(my_group - m // nb + nq, nq) * nb + lax.rem(m, nb)
        slot = (m // nb) * nb + my_slot
        return remote(
            tok_ref, tok_all.at[m // nb, block_of(my_slot), :], tok_s.at[m], tok_r.at[slot],
            {"ep": to},
        )

    def tok_arrival(m):
        return remote(
            tok_ref, tok_all.at[m // nb, block_of(lax.rem(m, nb)), :], tok_s.at[m], tok_r.at[m],
            {"ep": lax.rem(me + 1, nep)},
        )

    def out_copy(m):
        to = lax.rem(my_group + m // nb, nq) * nb + lax.rem(m, nb)
        return remote(
            out_send.at[m // nb, block_of(lax.rem(m, nb)), :], out_recv.at[me],
            out_s.at[m], out_r.at[me], {"ep": to},
        )

    def out_arrival(j):
        source = lax.rem(me + j, nep)
        return source, remote(
            out_send.at[0, block_of(0), :], out_recv.at[source],
            out_s.at[0], out_r.at[source], {"ep": source},
        )

    def ra_copy(k):
        return remote(ra.at[k], ra.at[k], ra_s.at[k], ra_r.at[k], {"tp": zl})

    def rb_copy(k):
        return remote(rb.at[k], rb.at[k], rb_s.at[k], rb_r.at[k], {"tp": zr})

    def ha_copy(k):
        return remote(ha.at[k], ha.at[k], ha_s.at[k], ha_r.at[k], {"tp": zr})

    def hb_copy(k):
        return remote(hb.at[k], hb.at[k], hb_s.at[k], hb_r.at[k], {"tp": zl})

    def send_tokens(m, carry):
        @pl.when(m != my_slot)
        def _():
            tok_copy(m).start()

        return carry

    lax.fori_loop(0, nep, send_tokens, 0)
    tok_all[0, block_of(my_slot), :] = tok_ref[...]

    def clear(j, carry):
        acc[j] = jnp.zeros(acc.shape[1:], acc.dtype)
        return carry

    lax.fori_loop(0, nq, clear, 0)

    before = (
        lax.broadcasted_iota(jnp.int32, (span, span), 0)
        < lax.broadcasted_iota(jnp.int32, (span, span), 1)
    ).astype(bf16)

    def row_ids(d, lanes):
        r = lax.broadcasted_iota(jnp.int32, (full, lanes), 0)
        mine = 2 * r + d
        lent = 2 * full - 1 - d - 2 * (r - half)
        return jnp.where(r < half, mine, lent).astype(f32)
    sub_id = lax.broadcasted_iota(jnp.int32, (16, span), 0)

    def prepare(q):
        def arrive(i, carry):
            m = q * nb + i

            @pl.when(m != my_slot)
            def _():
                tok_arrival(m).wait_recv()

            return carry

        lax.fori_loop(0, nb, arrive, 0)
        ids = meta_all[q, :top, :]
        fixed = meta_all[q, top:, :]
        chosen, wide = [], jnp.zeros((16, span), f32)
        for e in range(local):
            named = ids == me * local + e
            row = jnp.sum(named.astype(f32), axis=0, keepdims=True)
            weight = jnp.sum(jnp.where(named, fixed, 0), axis=0, keepdims=True)
            gate[q, e:e + 1, :] = weight.astype(f32) * (1.0 / 65536.0)
            wide = jnp.where(sub_id == e, row, wide)
            chosen.append(row)
        earlier = jnp.dot(wide.astype(bf16), before, preferred_element_type=f32)
        base = jnp.zeros((1, 1), f32)
        for e in range(local):
            place[q, e:e + 1, :] = jnp.where(
                chosen[e] > 0.5, base + earlier[e:e + 1, :], -1.0
            )
            base = base + jnp.sum(chosen[e], axis=1, keepdims=True)
            ends[q, e:e + 1, :] = jnp.broadcast_to(base, (1, LANES))

    def inside(k):
        return jnp.logical_and(k >= 0, k < chunks)

    def lend_copy(k, d):
        i = d * chunks + k
        return remote(sp_out.at[i], sp_in.at[i], sp_s.at[i], sp_r.at[i], {"ep": partner})

    def back_copy(k, d, hidden):
        i = d * chunks + k
        return remote(
            hidden.at[k, pl.ds(low_row, spill), :], hs_in.at[i], hs_s.at[i], hs_r.at[i],
            {"ep": partner},
        )

    def product_stage(k, d):
        @pl.when(inside(k))
        def _():
            q = k // ng
            g = lax.rem(k, ng)

            @pl.when(g == 0)
            def _():
                ids = row_ids(d, span)
                for e in range(local):
                    pick = ids == place[q, e:e + 1, :]
                    xbuf[d, e] = jnp.dot(
                        pick.astype(bf16), tok_all[q], preferred_element_type=f32
                    ).astype(bf16)

            total = jnp.dot(xbuf[d, 0], gu[g, 0], preferred_element_type=f32)
            for e in range(1, local):
                total += jnp.dot(xbuf[d, e], gu[g, e], preferred_element_type=f32)
            own[d, lax.rem(k, 2)] = total[:half]
            if spill:
                sp_out[d * chunks + k] = total[half:]
                lend_copy(k, d).start()

    def chain_stage(k, d, buf, copy, has_source, is_last, hidden):
        @pl.when(inside(k))
        def _():
            mine = own.at[d, lax.rem(k, 2)]
            if spill:
                lend_copy(k, d).wait_recv()
                mine[low_row:, :] += sp_in[d * chunks + k]

            @pl.when(has_source)
            def _():
                copy(k).wait_recv()
                mine[...] += buf[k].astype(f32)

            @pl.when(jnp.logical_not(is_last))
            def _():
                buf[k] = mine[...].astype(bf16)
                copy(k).start()

            @pl.when(is_last)
            def _():
                v = mine[:, :LANES]
                hidden[k] = (v / (1.0 + jnp.exp(-v)) * mine[:, LANES:]).astype(bf16)

    def hidden_stage(k, d, hidden, copy, has_source, is_last):
        @pl.when(inside(k))
        def _():
            @pl.when(has_source)
            def _():
                copy(k).wait_recv()

            @pl.when(jnp.logical_not(is_last))
            def _():
                copy(k).start()

            if spill:
                back_copy(k, d, hidden).start()

    def down_stage(k, d, hidden):
        @pl.when(inside(k))
        def _():
            if spill:
                back_copy(k, d, hidden).wait_recv()
            q = k // ng

            @pl.when(lax.rem(k, ng) == ng - 1)
            def _():
                units = jnp.concatenate([hidden[q * ng + g] for g in range(ng)], axis=1)
                if spill:
                    lent = jnp.concatenate(
                        [hs_in[d * chunks + q * ng + g] for g in range(ng)], axis=1
                    )
                    units = jnp.concatenate([units, lent], axis=0)
                at = row_ids(d, LANES)
                ids = row_ids(d, span)
                start = jnp.zeros((1, LANES), f32)
                result = jnp.zeros((full, dw.shape[1]), f32)
                spread = jnp.zeros((full, span), f32)
                scale = jnp.zeros((full, span), f32)
                for e in range(local):
                    end = ends[q, e:e + 1, :]
                    mine = jnp.logical_and(at >= start, at < end).astype(f32).astype(bf16)
                    start = end
                    result += lax.dot_general(
                        units * jnp.concatenate([mine] * ng, axis=1), dw[e],
                        (((1,), (1,)), ((), ())), preferred_element_type=f32,
                    )
                    pick = ids == place[q, e:e + 1, :]
                    spread = jnp.where(pick, 1.0, spread)
                    scale = jnp.where(pick, gate[q, e:e + 1, :], scale)
                scaled = result * jnp.sum(scale, axis=1, keepdims=True)
                high = scaled.astype(bf16)
                low = (scaled - high.astype(f32)).astype(bf16)
                spread = spread.astype(bf16)
                acc[q] += lax.dot_general(
                    jnp.concatenate([spread, spread], axis=0),
                    jnp.concatenate([high, low], axis=0),
                    (((0,), (0,)), ((), ())), preferred_element_type=f32,
                )

    turn = SKEW * (n - 1)
    from_right = SKEW * (n - 1 - z)
    from_left = SKEW * z
    lead = jnp.minimum(from_left, from_right)

    def step(t, carry):
        k_first = t - lead

        @pl.when(jnp.logical_and(inside(k_first), lax.rem(k_first, ng) == 0))
        def _():
            prepare(k_first // ng)

        @pl.when(jnp.logical_and(k_first >= 0, k_first < ng))
        def _():
            gate_copy(k_first).wait()
            up_copy(k_first).wait()

        @pl.when(t == turn + lead + 1)
        def _():
            down_copy.wait()

        product_stage(t - from_right, 0)
        product_stage(t - from_left, 1)
        chain_stage(t - 1 - from_right, 0, ra, ra_copy, z < n - 1, z == 0, ha)
        chain_stage(t - 1 - from_left, 1, rb, rb_copy, z > 0, z == n - 1, hb)
        hidden_stage(t - 1 - turn - from_left, 0, ha, ha_copy, z > 0, z == n - 1)
        hidden_stage(t - 1 - turn - from_right, 1, hb, hb_copy, z < n - 1, z == 0)
        down_stage(t - 2 - turn - from_left, 0, ha)
        down_stage(t - 2 - turn - from_right, 1, hb)
        k_done = t - 2 - turn - jnp.maximum(from_left, from_right)

        @pl.when(jnp.logical_and(inside(k_done), lax.rem(k_done, ng) == ng - 1))
        def _():
            q = k_done // ng
            out_send[q] = acc[q].astype(bf16)

            def give(i, carry):
                m = q * nb + i

                @pl.when(m != my_slot)
                def _():
                    out_copy(m).start()

                return carry

            lax.fori_loop(0, nb, give, 0)

        return carry

    lax.fori_loop(0, chunks + 2 * turn + 2, step, 0)

    def finish_chunk(k, carry):
        if spill:
            lend_copy(k, 0).wait_send()
            lend_copy(k, 1).wait_send()
            back_copy(k, 0, ha).wait_send()
            back_copy(k, 1, hb).wait_send()

        @pl.when(z > 0)
        def _():
            ra_copy(k).wait_send()
            hb_copy(k).wait_send()

        @pl.when(z < n - 1)
        def _():
            rb_copy(k).wait_send()
            ha_copy(k).wait_send()

        return carry

    lax.fori_loop(0, chunks, finish_chunk, 0)

    def finish_send(m, carry):
        @pl.when(m != my_slot)
        def _():
            tok_copy(m).wait_send()
            out_copy(m).wait_send()

        return carry

    lax.fori_loop(0, nep, finish_send, 0)
    own_rows = block_of(my_slot)

    def finish_block(j, carry):
        source, copy = out_arrival(j)
        copy.wait_recv()
        acc[0, own_rows, :] += out_recv[source].astype(f32)
        return carry

    lax.fori_loop(1, nep, finish_block, 0)
    out_ref[...] = acc[0, own_rows, :].astype(bf16)


def count_call(nep, nq, local, limits, meta):
    depth, rows = meta.shape
    nb = nep // nq
    dma = pltpu.SemaphoreType.DMA
    vmem = pl.BlockSpec(memory_space=pltpu.VMEM)
    shape = (nq, depth, nb * rows)
    return pl.pallas_call(
        functools.partial(count_kernel, nep, nq, local, depth // 2, limits),
        out_shape=(
            jax.ShapeDtypeStruct(shape, jnp.int32), jax.ShapeDtypeStruct((1,), jnp.int32)
        ),
        in_specs=[vmem],
        out_specs=(vmem, pl.BlockSpec(memory_space=pltpu.SMEM)),
        scratch_shapes=[pltpu.VMEM(shape, jnp.int32), dma((nep,)), dma((nep,))],
        compiler_params=pltpu.CompilerParams(collective_id=0, has_side_effects=True),
    )(meta)


def layer_call(nep, n, nq, top, full, half, number, tokens, meta_all, gate_weight, up_weight, down_weight):
    local, share, width = gate_weight.shape
    rows = tokens.shape[0]
    nb = nep // nq
    ng = width // LANES
    chunks = nq * ng
    spill = max(full - half, 16)
    lent = 2 * chunks if half < full else 1
    bf16, f32 = jnp.bfloat16, jnp.float32
    dma = pltpu.SemaphoreType.DMA
    vmem = pl.BlockSpec(memory_space=pltpu.VMEM)
    hbm = pl.BlockSpec(memory_space=pl.ANY)
    return pl.pallas_call(
        functools.partial(layer_kernel, nep, n, local, top, nq, full, half),
        out_shape=jax.ShapeDtypeStruct((rows, share), bf16),
        in_specs=[vmem, vmem, hbm, hbm, hbm],
        out_specs=vmem,
        scratch_shapes=[
            pltpu.VMEM((ng, local, share, 2 * LANES), bf16),
            pltpu.VMEM((local, share, width), bf16),
            pltpu.VMEM((nq, nb * rows, share), bf16),
            pltpu.VMEM((nq, 8, nb * rows), f32),
            pltpu.VMEM((nq, 8, nb * rows), f32),
            pltpu.VMEM((nq, 8, LANES), f32),
            pltpu.VMEM((2, local, full, share), bf16),
            pltpu.VMEM((2, 2, half, 2 * LANES), f32),
            pltpu.VMEM((chunks, half, 2 * LANES), bf16),
            pltpu.VMEM((chunks, half, 2 * LANES), bf16),
            pltpu.VMEM((chunks, half, LANES), bf16),
            pltpu.VMEM((chunks, half, LANES), bf16),
            pltpu.VMEM((lent, spill, 2 * LANES), f32),
            pltpu.VMEM((lent, spill, 2 * LANES), f32),
            pltpu.VMEM((lent, spill, LANES), bf16),
            pltpu.VMEM((nq, nb * rows, share), f32),
            pltpu.VMEM((nq, nb * rows, share), bf16),
            pltpu.VMEM((nep, rows, share), bf16),
            dma((2, ng)), dma,
            dma((nep,)), dma((nep,)),
            dma((chunks,)), dma((chunks,)), dma((chunks,)), dma((chunks,)),
            dma((chunks,)), dma((chunks,)), dma((chunks,)), dma((chunks,)),
            dma((lent,)), dma((lent,)), dma((lent,)), dma((lent,)),
            dma((nep,)), dma((nep,)),
        ],
        compiler_params=pltpu.CompilerParams(
            collective_id=number, has_side_effects=True, vmem_limit_bytes=60 * 1024 * 1024
        ),
    )(tokens, meta_all, gate_weight, up_weight, down_weight)


def on_device(nep, n, tokens, routing, gate_fixed, gate_weight, up_weight, down_weight):
    local = gate_weight.shape[0]
    rows, top = routing.shape
    cap = max(2, rows * top * 2 // (local * nep))
    nq = min(GROUPS, nep)
    full = nep // nq * local * cap // 2
    halves = [h for h in (full * s // 16 for s in SIZES) if h % 16 == 0] + [full]
    meta = jnp.concatenate([routing.T, gate_fixed.T], axis=0)
    meta_all, size = count_call(nep, nq, local, [4 * h for h in halves[:-1]], meta)
    calls = [
        functools.partial(layer_call, nep, n, nq, top, full, h, i + 1)
        for i, h in enumerate(halves)
    ]
    return lax.switch(
        size[0], calls, tokens, meta_all, gate_weight, up_weight, down_weight
    )


def solution(mesh):
    in_specs = (
        P("ep", "tp"),
        P("ep", None),
        P("ep", None),
        P("ep", "tp", None),
        P("ep", "tp", None),
        P("ep", "tp", None),
    )
    body = functools.partial(on_device, mesh.shape["ep"], mesh.shape["tp"])
    return jax.shard_map(
        body, mesh=mesh, in_specs=in_specs, out_specs=P("ep", "tp"), check_vma=False
    )
```

time: 141 us -> 112 us (0.79)
  Pallas kernels: 138 us -> 109 us
    pallas_call x1 -> x2, Pallas kernels: 138 us -> 109 us  [the longest x1 101 us: layer_call(): pl.pallas_call(functools.partial(layer_kernel, nep, n, local, top, nq, fu...]
where the time goes in v2:
time: 112 us; the launch traced here: 111 us
  Pallas kernels  109 us (97%)
  other arithmetic  1.3 us (1%)
    pallas_call x1, Pallas kernels, layer_call(): pl.pallas_call(functools.partial(layer_kernel, nep, n, local, top, nq, fu...  101 us
    pallas_call x1, Pallas kernels, count_call(): pl.pallas_call(functools.partial(count_kernel, nep, nq, local, depth // 2...  7.45 us

profile of v2, /device:TPU:1, one launch (start us, length us, event | category | flops | bytes accessed | tf_op | source)
XLA Modules:
  0.0 111.5 jit_solution(13152824796238390379)
XLA Ops:
  0.0 1.3 %pad_add_fusion.meta_ref = s32[16,128]{1,0:T(8,128)} fusion(s32[8,128]{1,0:T(8,128)} %bitcast.3, s32[8,128]{1,0:T(8,128)} %bitcast.4), kind=kLoop, calls=%fused_computation | loop fusion | flops 2048 | bytes 16384 | tf_op jit(solution)/shard_map/concatenate | solution.py:542
  1.3 7.5 %shard_map.67 = (s32[4,16,256]{2,1,0:T(8,128)S(1)}, s32[1]{0:T(128)}) custom-call(s32[16,128]{1,0:T(8,128)} %pad_add_fusion.meta_ref), custom_call_target="tpu_custom_call" | custom-call | tf_op jit(solution)/shard_map/pallas_call | solution.py:474
  9.4 101.4 %conditional.1 = (bf16[128,512]{1,0:T(8,128)(2,1)S(1)}) conditional(s32[]{:T(128)} %bitcast.2, (bf16[128,512]{1,0:T(8,128)(2,1)}, s32[4,16,256]{2,1,0:T(8,128)S(1)}, bf16[4,512,768]{2,1,0:T(8,128)(2,1)}, bf16[4,512,768]{2,1,0:T(8,128)(2,1)}, bf16[4,512,768]{2,1,0:T(8,128)(2,1)}) %tuple.14, (bf16[128,512]{1,0:T(8,128)(2,1)}, ...), branch_computations={%region_0.0_spmd, %region_1.0_spmd, %region_2.0_spmd} | conditional | bytes 8 | solution.py:548
  9.4 101.2 %branch_0_fun.1 = bf16[128,512]{1,0:T(8,128)(2,1)S(1)} custom-call(bf16[128,512]{1,0:T(8,128)(2,1)} %get-tuple-element.38.tok_ref, s32[4,16,256]{2,1,0:T(8,128)S(1)} %get-tuple-element.40.meta_all, bf16[4,512,768]{2,1,0:T(8,128)(2,1)} %get-tuple-element.41.gw_hbm, bf16[4,512,768]{2,1,0:T(8,128)(2,1)} %get-tuple-element.42.uw_hbm, ...), custom_call_target="tpu_custom_call" | custom-call | tf_op jit(solution)/shard_map/cond/branch_0_fun/pallas_call | solution.py:498
  110.8 0.7 copy.14

commit v3 on v2

--- a/solution.py
+++ b/solution.py
@@ -9,9 +9,11 @@
 
 MESH = pl.DeviceIdType.MESH
 SKEW = 2
+LEAD = 2
+LATE = 1
 GROUPS = 4
 LANES = 128
-SIZES = (10, 11)
+SIZES = (18, 19, 20, 21, 22)
 
 
 def remote(src, dst, s, r, device):
@@ -23,11 +25,12 @@
 
 def count_kernel(
     nep, nq, local, top, limits,
-    meta_ref, all_ref, size_ref, meta_all, meta_s, meta_r,
+    ids_ref, gate_ref, all_ref, size_ref, meta_ref, meta_all, meta_s, meta_r,
 ):
     me = lax.axis_index("ep")
     rows = meta_ref.shape[1]
     nb = nep // nq
+    span = nb * rows
     my_group = me // nb
     my_slot = lax.rem(me, nb)
     barrier = pltpu.get_barrier_semaphore()
@@ -39,6 +42,8 @@
         return carry
 
     lax.fori_loop(1, nep, greet, 0)
+    meta_ref[:top] = ids_ref[...]
+    meta_ref[top:] = gate_ref[...]
     pl.semaphore_wait(barrier, nep - 1)
 
     def block_of(i):
@@ -82,15 +87,17 @@
     lax.fori_loop(0, nep, start, 0)
     meta_all[0, :, block_of(my_slot)] = meta_ref[...]
     lax.fori_loop(0, nep, finish, 0)
-    worst = jnp.zeros((1, 1), jnp.float32)
+    chips = nep // 2
+    loads = jnp.zeros((nq * chips, span), jnp.float32)
+    line = lax.broadcasted_iota(jnp.int32, (nq * chips, span), 0)
     for q in range(nq):
         ids = meta_all[q, :top, :]
         all_ref[q] = meta_all[q]
-        for c in range(nep // 2):
+        for c in range(chips):
             here = jnp.logical_and(ids >= c * 2 * local, ids < (c + 1) * 2 * local)
             row = jnp.sum(here.astype(jnp.float32), axis=0, keepdims=True)
-            worst = jnp.maximum(worst, jnp.sum(row, axis=1, keepdims=True))
-    top_load = jnp.max(worst)
+            loads = jnp.where(line == q * chips + c, row, loads)
+    top_load = jnp.max(jnp.sum(loads, axis=1, keepdims=True))
     size = jnp.int32(0)
     for limit in limits:
         size += (top_load > float(limit)).astype(jnp.int32)
@@ -103,7 +110,7 @@
     tok_ref, meta_all, gw_hbm, uw_hbm, dw_hbm,
     out_ref,
     gu, dw, tok_all, place, gate, ends,
-    xbuf, own, ra, rb, ha, hb, sp_out, sp_in, hs_in, acc, out_send, out_recv,
+    xbuf, own, res, ra, rb, ha, hb, sp_out, sp_in, hs_in, acc, total_out, out_send, out_recv,
     gu_sem, dw_sem, tok_s, tok_r,
     ra_s, ra_r, rb_s, rb_r, ha_s, ha_r, hb_s, hb_r, sp_s, sp_r, hs_s, hs_r, out_s, out_r,
 ):
@@ -116,6 +123,8 @@
     nb = nep // nq
     span = nb * rows
     ng = gu.shape[0]
+    pair = ng // dw.shape[0]
+    late = pair if ng > pair else 0
     chunks = nq * ng
     bf16, f32 = jnp.bfloat16, jnp.float32
     zl = lax.rem(z + n - 1, n)
@@ -135,12 +144,16 @@
             gu.at[g, :, :, pl.ds(LANES, LANES)], gu_sem.at[1, g],
         )
 
-    down_copy = pltpu.make_async_copy(dw_hbm, dw, dw_sem)
+    def down_copy(i):
+        return pltpu.make_async_copy(
+            dw_hbm.at[:, :, pl.ds(i * pair * LANES, pair * LANES)], dw.at[i], dw_sem.at[i]
+        )
 
     for g in range(ng):
-        gate_copy(g).start()
-        up_copy(g).start()
-    down_copy.start()
+        gate_copy((g + late) % ng).start()
+        up_copy((g + late) % ng).start()
+    for i in range(ng // pair):
+        down_copy(i).start()
 
     barrier = pltpu.get_barrier_semaphore()
 
@@ -151,9 +164,16 @@
         return carry
 
     lax.fori_loop(1, nep, greet, 0)
-    for side in (zl, zr):
-        pl.semaphore_signal(barrier, inc=1, device_id={"tp": side}, device_id_type=MESH)
-    pl.semaphore_wait(barrier, nep + 1)
+
+    @pl.when(z > 0)
+    def _():
+        pl.semaphore_signal(barrier, inc=1, device_id={"tp": zl}, device_id_type=MESH)
+
+    @pl.when(z < n - 1)
+    def _():
+        pl.semaphore_signal(barrier, inc=1, device_id={"tp": zr}, device_id_type=MESH)
+
+    sides = (z > 0).astype(jnp.int32) + (z < n - 1).astype(jnp.int32)
 
     def block_of(i):
         return pl.ds(pl.multiple_of(i * rows, rows), rows)
@@ -198,22 +218,6 @@
     def hb_copy(k):
         return remote(hb.at[k], hb.at[k], hb_s.at[k], hb_r.at[k], {"tp": zl})
 
-    def send_tokens(m, carry):
-        @pl.when(m != my_slot)
-        def _():
-            tok_copy(m).start()
-
-        return carry
-
-    lax.fori_loop(0, nep, send_tokens, 0)
-    tok_all[0, block_of(my_slot), :] = tok_ref[...]
-
-    def clear(j, carry):
-        acc[j] = jnp.zeros(acc.shape[1:], acc.dtype)
-        return carry
-
-    lax.fori_loop(0, nq, clear, 0)
-
     before = (
         lax.broadcasted_iota(jnp.int32, (span, span), 0)
         < lax.broadcasted_iota(jnp.int32, (span, span), 1)
@@ -226,17 +230,19 @@
         return jnp.where(r < half, mine, lent).astype(f32)
     sub_id = lax.broadcasted_iota(jnp.int32, (16, span), 0)
 
+    def arrive(q):
+        def one(i, carry):
+            m = q * nb + i
+
+            @pl.when(m != my_slot)
+            def _():
+                tok_arrival(m).wait_recv()
+
+            return carry
+
+        lax.fori_loop(0, nb, one, 0)
+
     def prepare(q):
-        def arrive(i, carry):
-            m = q * nb + i
-
-            @pl.when(m != my_slot)
-            def _():
-                tok_arrival(m).wait_recv()
-
-            return carry
-
-        lax.fori_loop(0, nb, arrive, 0)
         ids = meta_all[q, :top, :]
         fixed = meta_all[q, top:, :]
         chosen, wide = [], jnp.zeros((16, span), f32)
@@ -256,8 +262,34 @@
             base = base + jnp.sum(chosen[e], axis=1, keepdims=True)
             ends[q, e:e + 1, :] = jnp.broadcast_to(base, (1, LANES))
 
+    prepare(0)
+    pl.semaphore_wait(barrier, nep - 1 + sides)
+
+    def send_tokens(m, carry):
+        @pl.when(m != my_slot)
+        def _():
+            tok_copy(m).start()
+
+        return carry
+
+    lax.fori_loop(0, nep, send_tokens, 0)
+    tok_all[0, block_of(my_slot), :] = tok_ref[...]
+
+    def clear(j, carry):
+        acc[j] = jnp.zeros(acc.shape[1:], acc.dtype)
+        return carry
+
+    lax.fori_loop(0, nq, clear, 0)
+
     def inside(k):
         return jnp.logical_and(k >= 0, k < chunks)
+
+    def decode(k):
+        c = lax.rem(k + late, chunks)
+        return c // ng, lax.rem(c, ng)
+
+    def spot(q, g):
+        return lax.rem(q * ng + g + chunks - late, chunks)
 
     def lend_copy(k, d):
         i = d * chunks + k
@@ -273,10 +305,9 @@
     def product_stage(k, d):
         @pl.when(inside(k))
         def _():
-            q = k // ng
-            g = lax.rem(k, ng)
-
-            @pl.when(g == 0)
+            q, g = decode(k)
+
+            @pl.when(jnp.logical_or(k == 0, g == 0))
             def _():
                 ids = row_ids(d, span)
                 for e in range(local):
@@ -288,7 +319,7 @@
             total = jnp.dot(xbuf[d, 0], gu[g, 0], preferred_element_type=f32)
             for e in range(1, local):
                 total += jnp.dot(xbuf[d, e], gu[g, e], preferred_element_type=f32)
-            own[d, lax.rem(k, 2)] = total[:half]
+            own[d, lax.rem(k, LEAD + 1)] = total[:half]
             if spill:
                 sp_out[d * chunks + k] = total[half:]
                 lend_copy(k, d).start()
@@ -296,7 +327,7 @@
     def chain_stage(k, d, buf, copy, has_source, is_last, hidden):
         @pl.when(inside(k))
         def _():
-            mine = own.at[d, lax.rem(k, 2)]
+            mine = own.at[d, lax.rem(k, LEAD + 1)]
             if spill:
                 lend_copy(k, d).wait_recv()
                 mine[low_row:, :] += sp_in[d * chunks + k]
@@ -304,17 +335,22 @@
             @pl.when(has_source)
             def _():
                 copy(k).wait_recv()
-                mine[...] += buf[k].astype(f32)
-
-            @pl.when(jnp.logical_not(is_last))
+
+            @pl.when(jnp.logical_and(has_source, jnp.logical_not(is_last)))
+            def _():
+                buf[k] = (mine[...] + buf[k].astype(f32)).astype(bf16)
+                copy(k).start()
+
+            @pl.when(jnp.logical_not(has_source))
             def _():
                 buf[k] = mine[...].astype(bf16)
                 copy(k).start()
 
             @pl.when(is_last)
             def _():
-                v = mine[:, :LANES]
-                hidden[k] = (v / (1.0 + jnp.exp(-v)) * mine[:, LANES:]).astype(bf16)
+                v = mine[:, :LANES] + buf[k, :, :LANES].astype(f32)
+                w = mine[:, LANES:] + buf[k, :, LANES:].astype(f32)
+                hidden[k] = (v / (1.0 + jnp.exp(-v)) * w).astype(bf16)
 
     def hidden_stage(k, d, hidden, copy, has_source, is_last):
         @pl.when(inside(k))
@@ -335,42 +371,62 @@
         def _():
             if spill:
                 back_copy(k, d, hidden).wait_recv()
-            q = k // ng
-
-            @pl.when(lax.rem(k, ng) == ng - 1)
-            def _():
-                units = jnp.concatenate([hidden[q * ng + g] for g in range(ng)], axis=1)
+            q, g = decode(k)
+            home = (q == 0).astype(jnp.int32)
+
+            @pl.when(lax.rem(g, pair) == pair - 1)
+            def _():
+                parts = [spot(q, g - pair + 1 + i) for i in range(pair)]
+                units = jnp.concatenate([hidden[i] for i in parts], axis=1)
                 if spill:
-                    lent = jnp.concatenate(
-                        [hs_in[d * chunks + q * ng + g] for g in range(ng)], axis=1
-                    )
+                    lent = jnp.concatenate([hs_in[d * chunks + i] for i in parts], axis=1)
                     units = jnp.concatenate([units, lent], axis=0)
                 at = row_ids(d, LANES)
-                ids = row_ids(d, span)
                 start = jnp.zeros((1, LANES), f32)
-                result = jnp.zeros((full, dw.shape[1]), f32)
-                spread = jnp.zeros((full, span), f32)
-                scale = jnp.zeros((full, span), f32)
+                result = jnp.zeros((dw.shape[2], full), f32)
                 for e in range(local):
                     end = ends[q, e:e + 1, :]
                     mine = jnp.logical_and(at >= start, at < end).astype(f32).astype(bf16)
                     start = end
                     result += lax.dot_general(
-                        units * jnp.concatenate([mine] * ng, axis=1), dw[e],
+                        dw[g // pair, e], units * jnp.concatenate([mine] * pair, axis=1),
                         (((1,), (1,)), ((), ())), preferred_element_type=f32,
                     )
+                first = jnp.logical_or(
+                    k == pair - 1, jnp.logical_and(q > 0, g == pair - 1)
+                )
+
+                @pl.when(first)
+                def _():
+                    res[d, home] = result
+
+                @pl.when(jnp.logical_not(first))
+                def _():
+                    res[d, home] += result
+
+            @pl.when(complete(k))
+            def _():
+                ids = row_ids(d, span)
+                top_part = jnp.zeros((full, span), f32)
+                for e in range(local):
                     pick = ids == place[q, e:e + 1, :]
-                    spread = jnp.where(pick, 1.0, spread)
-                    scale = jnp.where(pick, gate[q, e:e + 1, :], scale)
-                scaled = result * jnp.sum(scale, axis=1, keepdims=True)
-                high = scaled.astype(bf16)
-                low = (scaled - high.astype(f32)).astype(bf16)
-                spread = spread.astype(bf16)
-                acc[q] += lax.dot_general(
-                    jnp.concatenate([spread, spread], axis=0),
-                    jnp.concatenate([high, low], axis=0),
-                    (((0,), (0,)), ((), ())), preferred_element_type=f32,
+                    top_part = jnp.where(pick, gate[q, e:e + 1, :], top_part)
+                coarse = top_part.astype(bf16)
+                fine = (top_part - coarse.astype(f32)).astype(bf16)
+                value = res[d, home]
+                high = value.astype(bf16)
+                low = (value - high.astype(f32)).astype(bf16)
+                acc[q] += jnp.dot(
+                    jnp.concatenate([high, high, low], axis=1),
+                    jnp.concatenate([coarse, fine, coarse], axis=0),
+                    preferred_element_type=f32,
                 )
+
+    def complete(k):
+        q, g = decode(k)
+        if late == 0:
+            return g == ng - 1
+        return jnp.logical_or(k == chunks - 1, jnp.logical_and(q > 0, g == ng - 1))
 
     turn = SKEW * (n - 1)
     from_right = SKEW * (n - 1 - z)
@@ -379,34 +435,38 @@
 
     def step(t, carry):
         k_first = t - lead
-
-        @pl.when(jnp.logical_and(inside(k_first), lax.rem(k_first, ng) == 0))
-        def _():
-            prepare(k_first // ng)
-
-        @pl.when(jnp.logical_and(k_first >= 0, k_first < ng))
-        def _():
-            gate_copy(k_first).wait()
-            up_copy(k_first).wait()
-
-        @pl.when(t == turn + lead + 1)
-        def _():
-            down_copy.wait()
-
+        q_first, g_first = decode(k_first)
+
+        @pl.when(jnp.logical_and(inside(k_first), jnp.logical_and(q_first > 0, g_first == 0)))
+        def _():
+            prepare(q_first)
+            arrive(q_first)
+
+        @pl.when(jnp.logical_and(inside(k_first), k_first < ng))
+        def _():
+            gate_copy(g_first).wait()
+            up_copy(g_first).wait()
+
+        @pl.when(t == LEAD + LATE + turn + lead + pair - 1)
+        def _():
+            for i in range(ng // pair):
+                down_copy(i).wait()
+
+        back = t - LEAD - turn
+        chain_stage(t - LEAD - from_right, 0, ra, ra_copy, z < n - 1, z == 0, ha)
+        chain_stage(t - LEAD - from_left, 1, rb, rb_copy, z > 0, z == n - 1, hb)
+        hidden_stage(back - from_left, 0, ha, ha_copy, z > 0, z == n - 1)
+        hidden_stage(back - from_right, 1, hb, hb_copy, z < n - 1, z == 0)
         product_stage(t - from_right, 0)
         product_stage(t - from_left, 1)
-        chain_stage(t - 1 - from_right, 0, ra, ra_copy, z < n - 1, z == 0, ha)
-        chain_stage(t - 1 - from_left, 1, rb, rb_copy, z > 0, z == n - 1, hb)
-        hidden_stage(t - 1 - turn - from_left, 0, ha, ha_copy, z > 0, z == n - 1)
-        hidden_stage(t - 1 - turn - from_right, 1, hb, hb_copy, z < n - 1, z == 0)
-        down_stage(t - 2 - turn - from_left, 0, ha)
-        down_stage(t - 2 - turn - from_right, 1, hb)
-        k_done = t - 2 - turn - jnp.maximum(from_left, from_right)
-
-        @pl.when(jnp.logical_and(inside(k_done), lax.rem(k_done, ng) == ng - 1))
-        def _():
-            q = k_done // ng
-            out_send[q] = acc[q].astype(bf16)
+        down_stage(back - LATE - from_left, 0, ha)
+        down_stage(back - LATE - from_right, 1, hb)
+        k_done = back - LATE - jnp.maximum(from_left, from_right)
+
+        @pl.when(jnp.logical_and(inside(k_done), complete(k_done)))
+        def _():
+            q, _ = decode(k_done)
+            out_send[q] = acc[q].T.astype(bf16)
 
             def give(i, carry):
                 m = q * nb + i
@@ -421,7 +481,8 @@
 
         return carry
 
-    lax.fori_loop(0, chunks + 2 * turn + 2, step, 0)
+    arrive(0)
+    lax.fori_loop(0, chunks + 2 * turn + LEAD + LATE, step, 0)
 
     def finish_chunk(k, carry):
         if spill:
@@ -453,34 +514,38 @@
         return carry
 
     lax.fori_loop(0, nep, finish_send, 0)
-    own_rows = block_of(my_slot)
+    total_out[...] = acc[0, :, block_of(my_slot)].T
 
     def finish_block(j, carry):
         source, copy = out_arrival(j)
         copy.wait_recv()
-        acc[0, own_rows, :] += out_recv[source].astype(f32)
+        total_out[...] += out_recv[source].astype(f32)
         return carry
 
     lax.fori_loop(1, nep, finish_block, 0)
-    out_ref[...] = acc[0, own_rows, :].astype(bf16)
-
-
-def count_call(nep, nq, local, limits, meta):
-    depth, rows = meta.shape
+    out_ref[...] = total_out[...].astype(bf16)
+
+
+def count_call(nep, nq, local, limits, routing, gate_fixed):
+    rows, top = routing.shape
+    depth = 2 * top
     nb = nep // nq
     dma = pltpu.SemaphoreType.DMA
     vmem = pl.BlockSpec(memory_space=pltpu.VMEM)
     shape = (nq, depth, nb * rows)
     return pl.pallas_call(
-        functools.partial(count_kernel, nep, nq, local, depth // 2, limits),
+        functools.partial(count_kernel, nep, nq, local, top, limits),
         out_shape=(
             jax.ShapeDtypeStruct(shape, jnp.int32), jax.ShapeDtypeStruct((1,), jnp.int32)
         ),
-        in_specs=[vmem],
+        in_specs=[vmem, vmem],
         out_specs=(vmem, pl.BlockSpec(memory_space=pltpu.SMEM)),
-        scratch_shapes=[pltpu.VMEM(shape, jnp.int32), dma((nep,)), dma((nep,))],
+        scratch_shapes=[
+            pltpu.VMEM((depth, rows), jnp.int32), pltpu.VMEM(shape, jnp.int32),
+            dma((nep,)), dma((nep,)),
+        ],
         compiler_params=pltpu.CompilerParams(collective_id=0, has_side_effects=True),
-    )(meta)
+    )(routing.T, gate_fixed.T)
 
 
 def layer_call(nep, n, nq, top, full, half, number, tokens, meta_all, gate_weight, up_weight, down_weight):
@@ -489,6 +554,7 @@
     nb = nep // nq
     ng = width // LANES
     chunks = nq * ng
+    pair = 2 if ng % 2 == 0 else 1
     spill = max(full - half, 16)
     lent = 2 * chunks if half < full else 1
     bf16, f32 = jnp.bfloat16, jnp.float32
@@ -502,13 +568,14 @@
         out_specs=vmem,
         scratch_shapes=[
             pltpu.VMEM((ng, local, share, 2 * LANES), bf16),
-            pltpu.VMEM((local, share, width), bf16),
+            pltpu.VMEM((ng // pair, local, share, pair * LANES), bf16),
             pltpu.VMEM((nq, nb * rows, share), bf16),
             pltpu.VMEM((nq, 8, nb * rows), f32),
             pltpu.VMEM((nq, 8, nb * rows), f32),
             pltpu.VMEM((nq, 8, LANES), f32),
             pltpu.VMEM((2, local, full, share), bf16),
-            pltpu.VMEM((2, 2, half, 2 * LANES), f32),
+            pltpu.VMEM((2, LEAD + 1, half, 2 * LANES), f32),
+            pltpu.VMEM((2, 2, share, full), f32),
             pltpu.VMEM((chunks, half, 2 * LANES), bf16),
             pltpu.VMEM((chunks, half, 2 * LANES), bf16),
             pltpu.VMEM((chunks, half, LANES), bf16),
@@ -516,10 +583,11 @@
             pltpu.VMEM((lent, spill, 2 * LANES), f32),
             pltpu.VMEM((lent, spill, 2 * LANES), f32),
             pltpu.VMEM((lent, spill, LANES), bf16),
-            pltpu.VMEM((nq, nb * rows, share), f32),
+            pltpu.VMEM((nq, share, nb * rows), f32),
+            pltpu.VMEM((rows, share), f32),
             pltpu.VMEM((nq, nb * rows, share), bf16),
             pltpu.VMEM((nep, rows, share), bf16),
-            dma((2, ng)), dma,
+            dma((2, ng)), dma((ng // pair,)),
             dma((nep,)), dma((nep,)),
             dma((chunks,)), dma((chunks,)), dma((chunks,)), dma((chunks,)),
             dma((chunks,)), dma((chunks,)), dma((chunks,)), dma((chunks,)),
@@ -538,9 +606,10 @@
     cap = max(2, rows * top * 2 // (local * nep))
     nq = min(GROUPS, nep)
     full = nep // nq * local * cap // 2
-    halves = [h for h in (full * s // 16 for s in SIZES) if h % 16 == 0] + [full]
-    meta = jnp.concatenate([routing.T, gate_fixed.T], axis=0)
-    meta_all, size = count_call(nep, nq, local, [4 * h for h in halves[:-1]], meta)
+    halves = [h for h in (full * s // 32 for s in SIZES) if h % 8 == 0] + [full]
+    meta_all, size = count_call(
+        nep, nq, local, [4 * h for h in halves[:-1]], routing, gate_fixed
+    )
     calls = [
         functools.partial(layer_call, nep, n, nq, top, full, h, i + 1)
         for i, h in enumerate(halves)

time: 112 us -> 107 us (0.955)
  Pallas kernels: 109 us -> 105 us
  other arithmetic: 1.3 us -> 0 us
    pallas_call x1, Pallas kernels: 101 us -> 97.5 us  [layer_call(): pl.pallas_call(functools.partial(layer_kernel, nep, n, local, top, nq, fu...]
    concatenate x1 -> x0, other arithmetic: 1.3 us -> none  [on_device(): meta = jnp.concatenate([routing.T, gate_fixed.T], axis=0)]
where the time goes in v3:
time: 107 us
  Pallas kernels  105 us (98%)
    pallas_call x1, Pallas kernels, layer_call(): pl.pallas_call(functools.partial(layer_kernel, nep, n, local, top, nq, fu...  97.5 us
    pallas_call x1, Pallas kernels, count_call(): pl.pallas_call(functools.partial(count_kernel, nep, nq, local, top, limit...  7.47 us

profile of v3, /device:TPU:1, one launch (start us, length us, event | category | flops | bytes accessed | tf_op | source)
XLA Modules:
  0.0 106.9 jit_solution(8127172838069364212)
XLA Ops:
  0.0 7.5 %shard_map.70 = (s32[4,16,256]{2,1,0:T(8,128)S(1)}, s32[1]{0:T(128)}) custom-call(s32[8,128]{1,0:T(8,128)} %bitcast.3, s32[8,128]{1,0:T(8,128)} %bitcast.4), custom_call_target="tpu_custom_call" | custom-call | tf_op jit(solution)/shard_map/pallas_call | solution.py:536
  8.1 98.1 %conditional.1 = (bf16[128,512]{1,0:T(8,128)(2,1)S(1)}) conditional(s32[]{:T(128)} %bitcast.2, (bf16[128,512]{1,0:T(8,128)(2,1)}, s32[4,16,256]{2,1,0:T(8,128)S(1)}, bf16[4,512,768]{2,1,0:T(8,128)(2,1)}, bf16[4,512,768]{2,1,0:T(8,128)(2,1)}, bf16[4,512,768]{2,1,0:T(8,128)(2,1)}) %tuple.23, ...), branch_computations={%region_0.0_spmd, %region_1.0_spmd, %region_2.0_spmd, %region_3.0_... | conditional | bytes 8 | solution.py:617
  8.2 97.5 %branch_2_fun.1 = bf16[128,512]{1,0:T(8,128)(2,1)S(1)} custom-call(bf16[128,512]{1,0:T(8,128)(2,1)} %get-tuple-element.82.tok_ref, s32[4,16,256]{2,1,0:T(8,128)S(1)} %get-tuple-element.83.meta_all, bf16[4,512,768]{2,1,0:T(8,128)(2,1)} %get-tuple-element.84.gw_hbm, bf16[4,512,768]{2,1,0:T(8,128)(2,1)} %get-tuple-element.85.uw_hbm, ...), custom_call_target="tpu_custom_call" | custom-call | tf_op jit(solution)/shard_map/cond/branch_2_fun/pallas_call | solution.py:564
  106.2 0.7 copy.20
